TPU v7x, 32 devices: a whole 2x2x4 slice. The times are simulated.
32 devices in a mesh: dp: 8 (over y, x, core), mp: 4 (over z).
Axes of the slice: x: 2, y: 2, z: 4, core: 2. Of those that a mesh axis runs over, the one named last changes fastest.
Arguments:
- feature_ids: int32 [8, 2048, 8], P('dp'), may hold values from 0 to 4095
- tables: bfloat16 [8, 4096, 128], P('dp'), may hold values from -5 to 5
- table_of_feature: int32 [8], replicated, may hold values from 0 to 7, each once
- cross_down: bfloat16 [2, 1024, 512], P(None, 'mp'), may hold values from -0.1875 to 0.1875
- cross_up: bfloat16 [2, 1024, 512], P(None, 'mp'), may hold values from -0.125 to 0.125
- cross_bias: float32 [2, 1024], P(None, 'mp'), may hold values from -3 to 3
- tower_weight: bfloat16 [1024, 2048], P('dp', 'mp'), may hold values from -0.1875 to 0.1875
- tower_bias: float32 [2048], P('mp'), may hold values from -3 to 3
Outputs:
- hidden: bfloat16 [2048, 2048], P('dp', 'mp')
Inputs may be any that keep to these rules, and one draw needn't show every extreme that they name: `feature_ids`: each id indexes a row of its own table. `table_of_feature`: each table serves exactly one feature.
All inputs are finite; a program needn't handle non-finite values.
Results may differ from a plain program's by a relative error of at most 0.015.
Values may be sent and summed in bfloat16 or wider, within the bound.
A program may use at most 64 MiB of HBM per device.

v0:
```python
import jax
import jax.numpy as jnp
from jax import lax
from jax.sharding import PartitionSpec as P


def body(
    feature_ids,
    tables,
    table_of_feature,
    cross_down,
    cross_up,
    cross_bias,
    tower_weight,
    tower_bias,
):
    groups = lax.axis_size("dp")
    members = lax.axis_size("mp")
    member = lax.axis_index("mp")
    table_count, batch_size, hot_count = feature_ids.shape
    row_count = batch_size // (groups * members)
    shaped = feature_ids[0].reshape(groups, members, row_count, hot_count)
    own_ids = lax.dynamic_index_in_dim(shaped, member, 1, keepdims=False).reshape(
        groups * row_count, hot_count
    )
    summed = jnp.zeros((groups * row_count, tables.shape[2]), jnp.float32)
    for hot_index in range(hot_count):
        summed = summed + jnp.take(tables[0], own_ids[:, hot_index], axis=0).astype(jnp.float32)
    columns = [summed.astype(jnp.bfloat16)]
    pooled = jnp.stack(columns, axis=1)
    regrouped = lax.all_to_all(pooled, "dp", split_axis=0, concat_axis=1, tiled=True)
    ordered = jnp.take(regrouped, table_of_feature, axis=1)
    by_width = lax.all_to_all(ordered, "mp", split_axis=1, concat_axis=0, tiled=True)
    group_rows = by_width.shape[0]
    embedded = by_width.reshape(group_rows, -1)
    embedded_wide = embedded.astype(jnp.float32)
    crossed = embedded
    layer_total = cross_down.shape[0]
    for layer_index in range(layer_total):
        partial_value = jnp.dot(
            crossed, cross_down[layer_index], preferred_element_type=jnp.float32
        )
        projected = lax.psum(partial_value.astype(jnp.bfloat16), "mp")
        lifted = lax.dot_general(
            projected,
            cross_up[layer_index],
            (((1,), (1,)), ((), ())),
            preferred_element_type=jnp.float32,
        )
        crossed = (
            embedded_wide * (lifted + cross_bias[layer_index]) + crossed.astype(jnp.float32)
        ).astype(jnp.bfloat16)
    full_rows = lax.all_gather(crossed, "mp", axis=1, tiled=True)
    pre_act = jnp.dot(
        full_rows,
        lax.all_gather(tower_weight, "dp", axis=0, tiled=True),
        preferred_element_type=jnp.float32,
    )
    return jax.nn.relu(pre_act + tower_bias).astype(jnp.bfloat16)


def solution(mesh):
    return jax.shard_map(
        body,
        mesh=mesh,
        in_specs=(
            P("dp", None, None),
            P("dp", None, None),
            P(),
            P(None, "mp", None),
            P(None, "mp", None),
            P(None, "mp"),
            P("dp", "mp"),
            P("mp"),
        ),
        out_specs=P("dp", "mp"),
        check_vma=False,
    )
```

profile of v0, /device:TPU:0, one launch (start us, length us, event | category | flops | bytes accessed | tf_op | source)
XLA Modules:
  0.0 143.6 jit_solution(9518459660529289800)
XLA Ops:
  7.4 1.0 reshape_squeeze.3
  8.8 1.3 gather_fusion.2
  10.2 1.3 gather_fusion.3
  11.5 1.3 gather_fusion.4
  12.9 1.3 gather_fusion.5
  14.2 1.3 gather_fusion.6
  15.6 1.3 gather_fusion.7
  17.0 1.3 gather_fusion.8
  18.3 1.3 gather_fusion.1
  19.7 0.8 fusion.16
  21.0 0.7 reduce.4
  21.7 0.7 reshape.125
  22.3 5.3 %all-to-all-start = ((bf16[8,2,4096]{2,1,0:T(2,128)(2,1)}), bf16[8,2,4096]{2,1,0:T(2,128)(2,1)S(1)}, u32[]{:S(2)}, u32[]{:S(2)}) async-start(bf16[8,2,4096]{2,1,0:T(2,128)(2,1)} %reshape.125), calls=%async_computation | async-start | bytes 262144 | tf_op jit(solution)/shard_map/all_to_all | solution.py:31
  27.8 5.4 %all-to-all-done = bf16[8,2,4096]{2,1,0:T(2,128)(2,1)S(1)} async-done(((bf16[8,2,4096]{2,1,0:T(2,128)(2,1)}), bf16[8,2,4096]{2,1,0:T(2,128)(2,1)S(1)}, u32[]{:S(2)}, u32[]{:S(2)}) %all-to-all-start) | async-done | bytes 131104 | tf_op jit(solution)/shard_map/all_to_all | solution.py:31
  34.0 10.6 %all_to_all.33 = bf16[64,8,128]{2,0,1:T(8,128)(2,1)S(1)} all-to-all(bf16[64,8,128]{2,0,1:T(8,128)(2,1)S(1)} %select_bitcast_fusion), channel_id=1, replica_groups=mesh['dp'=8,'mp'=4] {'mp'}, dimensions={1} | all-to-all | bytes 262144 | tf_op jit(solution)/shard_map/all_to_all | solution.py:33
  44.8 0.9 convolution_convert_fusion.1
  45.8 0.6 copy-done.2
  46.4 32.4 %all-reduce.3.cloned.1.call-done = bf16[256,512]{1,0:T(8,128)(2,1)} async-done(((bf16[256,512]{1,0:T(8,128)(2,1)}), bf16[256,512]{1,0:T(8,128)(2,1)}) %all-reduce.3.cloned.1.call-update) | async-done | bytes 262160 | tf_op jit(solution)/shard_map/psum | solution.py:43
  78.8 1.2 fusion.6
  80.0 0.9 convolution_convert_fusion
  81.5 35.1 %all-reduce.5.cloned.1.call-done = bf16[256,512]{1,0:T(8,128)(2,1)} async-done(((bf16[256,512]{1,0:T(8,128)(2,1)}), bf16[256,512]{1,0:T(8,128)(2,1)}) %all-reduce.5.cloned.1.call-update) | async-done | bytes 262160 | tf_op jit(solution)/shard_map/psum | solution.py:43
  116.6 1.2 fusion.7
  117.8 16.0 %all_gather.6 = bf16[256,1024]{1,0:T(8,128)(2,1)S(1)} all-gather(bf16[256,256]{1,0:T(8,128)(2,1)S(1)} %fusion.7), channel_id=1, replica_groups=mesh['dp'=8,'mp'=4] {'mp'}, dimensions={1}, use_global_device_ids=true | all-gather | bytes 655360 | tf_op jit(solution)/shard_map/all_gather | solution.py:53
  133.8 2.4 %fusion.1 = bf16[256,512]{1,0:T(8,128)(2,1)} fusion(bf16[256,1024]{1,0:T(8,128)(2,1)S(1)} %all_gather.6, bf16[1024,512]{1,0:T(8,128)(2,1)} %all-gather.2.cloned.1.call-done, f32[512]{0:T(512)S(1)} %copy-done.4), kind=kOutput, calls=%fused_computation.11 | convolution fusion | flops 268828672 | bytes 1837056 | tf_op jit(solution)/shard_map/dot_general | solution.py:54
  (51 shorter events, 2.5 us)
Async XLA Ops:
  7.4 1.4 %copy-start = (bf16[1,4096,128]{2,1,0:T(8,128)(2,1)S(1)}, bf16[1,4096,128]{2,1,0:T(8,128)(2,1)}, u32[]{:S(2)}) copy-start(bf16[1,4096,128]{2,1,0:T(8,128)(2,1)} %param.11) | copy-start | bytes 3145732
  22.3 5.4 %copy-start.5 = (s32[8]{0:T(128)S(1)}, s32[8]{0:T(128)}, u32[]{:S(2)}) copy-start(s32[8]{0:T(128)} %param.12) | copy-start | bytes 100
  22.3 10.8 %all-to-all-start = ((bf16[8,2,4096]{2,1,0:T(2,128)(2,1)}), bf16[8,2,4096]{2,1,0:T(2,128)(2,1)S(1)}, u32[]{:S(2)}, u32[]{:S(2)}) async-start(bf16[8,2,4096]{2,1,0:T(2,128)(2,1)} %reshape.125), calls=%async_computation | async-start | bytes 262144 | tf_op jit(solution)/shard_map/all_to_all | solution.py:31
  27.7 51.1 %all-reduce.3.cloned.1.call-start = ((), (), s32[]{:S(2)}) async-start(), calls=%async_computation.2 | async-start | bytes 524288 | tf_op jit(solution)/shard_map/psum | solution.py:43
  33.3 11.5 %copy-start.1 = (bf16[2,256,512]{2,1,0:T(8,128)(2,1)S(1)}, bf16[2,256,512]{2,1,0:T(8,128)(2,1)}, u32[]{:S(2)}) copy-start(bf16[2,256,512]{2,1,0:T(8,128)(2,1)} %param.13) | copy-start | bytes 1572868
  44.8 34.0 %copy-start.3 = (bf16[2,256,512]{2,1,0:T(8,128)(2,1)S(1)}, bf16[2,256,512]{2,1,0:T(8,128)(2,1)}, u32[]{:S(2)}) copy-start(bf16[2,256,512]{2,1,0:T(8,128)(2,1)} %param.14) | copy-start | bytes 1572868
  45.7 0.7 copy-start.2
  45.8 70.8 %all-reduce.5.cloned.1.call-start = ((), (), s32[]{:S(2)}) async-start(), calls=%async_computation.3 | async-start | bytes 524288 | tf_op jit(solution)/shard_map/psum | solution.py:43
  81.0 52.8 %all-gather.2.cloned.1.call-start = ((), (), s32[]{:S(2)}) async-start(), calls=%async_computation.4 | async-start | bytes 1179648 | tf_op jit(solution)/shard_map/all_gather | solution.py:56
  117.8 16.0 %copy-start.4 = (f32[512]{0:T(512)S(1)}, f32[512]{0:T(512)}, u32[]{:S(2)}) copy-start(f32[512]{0:T(512)} %param.17) | copy-start | bytes 6148
Sparse Core Ops, SparseCore 0:
  45.9 32.8 all-reduce.2
  81.1 35.4 all-reduce.4
Sparse Core Ops, SparseCore 1:
  83.3 23.1 all-gather.1
where the time goes:
time: 144 us
  waiting for transfers between devices  73.4 us (51%)
  blocking collectives  26.6 us (18%)
  between operations  15.2 us (11%)
  local copies, waits for them, and re-layouts  14.7 us (10%)
  matrix products  6.65 us (5%)
  starting transfers between devices  5.45 us (4%)
  other arithmetic  1.66 us (1%)
    psum x2, waiting for transfers between devices, body(): projected = lax.psum(partial_value.astype(jnp.bfloat16), 'mp')  67.4 us
    all_gather x1, blocking collectives, body(): full_rows = lax.all_gather(crossed, 'mp', axis=1, tiled=True)  16 us
    gather x8, local copies, waits for them, and re-layouts, body(): jnp.take(tables[0], own_ids[:, hot_index], axis=0).astype(jnp.float32)  10.7 us
    all_to_all x1, blocking collectives, body(): lax.all_to_all(ordered, 'mp', split_axis=1, concat_axis=0, tiled=True)  10.6 us
    all_to_all x1, waiting for transfers between devices, body(): lax.all_to_all(pooled, 'dp', split_axis=0, concat_axis=1, tiled=True)  5.4 us
    all_to_all x1, starting transfers between devices, body(): lax.all_to_all(pooled, 'dp', split_axis=0, concat_axis=1, tiled=True)  5.33 us
  transfers between devices with their start and end apart: 4, of which 3 were waited for; matrix products, arithmetic and copies ran while one was open for 1% of the time, Pallas kernels for 0%

commit v1 on v0

--- a/solution.py
+++ b/solution.py
@@ -28,7 +28,9 @@
         summed = summed + jnp.take(tables[0], own_ids[:, hot_index], axis=0).astype(jnp.float32)
     columns = [summed.astype(jnp.bfloat16)]
     pooled = jnp.stack(columns, axis=1)
-    regrouped = lax.all_to_all(pooled, "dp", split_axis=0, concat_axis=1, tiled=True)
+    pieces = jnp.split(pooled, lax.axis_size("dp"), axis=0)
+    received = lax.all_to_all(jnp.stack(pieces), "dp", 0, 0)
+    regrouped = jnp.concatenate(received, axis=1)
     ordered = jnp.take(regrouped, table_of_feature, axis=1)
     by_width = lax.all_to_all(ordered, "mp", split_axis=1, concat_axis=0, tiled=True)
     group_rows = by_width.shape[0]

time: 144 us -> 147 us (1.021)
  local copies, waits for them, and re-layouts: 14.7 us -> 18.2 us
    unnamed x15 -> x19, local copies, waits for them, and re-layouts: 1.47 us -> 4.88 us
where the time goes in v1:
time: 147 us; the launch traced here: 146 us
  waiting for transfers between devices  73.3 us (50%)
  blocking collectives  26.6 us (18%)
  local copies, waits for them, and re-layouts  18.2 us (12%)
  between operations  15.2 us (10%)
  matrix products  6.67 us (5%)
  starting transfers between devices  5.45 us (4%)
    psum x2, waiting for transfers between devices, body(): projected = lax.psum(partial_value.astype(jnp.bfloat16), 'mp')  67.4 us
    all_gather x1, blocking collectives, body(): full_rows = lax.all_gather(crossed, 'mp', axis=1, tiled=True)  16 us
    gather x8, local copies, waits for them, and re-layouts, body(): jnp.take(tables[0], own_ids[:, hot_index], axis=0).astype(jnp.float32)  10.7 us
    all_to_all x1, blocking collectives, body(): lax.all_to_all(ordered, 'mp', split_axis=1, concat_axis=0, tiled=True)  10.6 us
    all_to_all x1, waiting for transfers between devices, body(): received = lax.all_to_all(jnp.stack(pieces), 'dp', 0, 0)  5.4 us
    all_to_all x1, starting transfers between devices, body(): received = lax.all_to_all(jnp.stack(pieces), 'dp', 0, 0)  5.33 us
    unnamed x19, local copies, waits for them, and re-layouts  4.88 us
  transfers between devices with their start and end apart: 4, of which 3 were waited for; matrix products, arithmetic and copies ran while one was open for 1% of the time, Pallas kernels for 0%

profile of v1, /device:TPU:0, one launch (start us, length us, event | category | flops | bytes accessed | tf_op | source)
XLA Modules:
  0.0 146.3 jit_solution(5905630463273590076)
XLA Ops:
  7.4 1.0 reshape_squeeze.3
  8.8 1.3 gather_fusion.2
  10.2 1.3 gather_fusion.3
  11.5 1.3 gather_fusion.4
  12.9 1.3 gather_fusion.5
  14.2 1.3 gather_fusion.6
  15.6 1.3 gather_fusion.1
  16.9 1.3 gather_fusion.7
  18.3 1.3 gather_fusion.8
  19.6 0.8 add_convert_fusion
  20.4 0.6 fusion.25
  21.0 0.6 fusion.24
  21.6 0.6 fusion.23
  25.3 5.3 %all-to-all-start = ((bf16[8,64,1,128]{3,1,2,0:T(8,128)(2,1)}), bf16[8,64,1,128]{3,1,2,0:T(8,128)(2,1)S(1)}, u32[]{:S(2)}, u32[]{:S(2)}) async-start(bf16[8,64,1,128]{3,1,2,0:T(8,128)(2,1)} %fusion.18), calls=%async_computation | async-start | bytes 262144 | tf_op jit(solution)/shard_map/all_to_all | solution.py:32
  30.7 5.4 %all-to-all-done = bf16[8,64,1,128]{3,1,2,0:T(8,128)(2,1)S(1)} async-done(((bf16[8,64,1,128]{3,1,2,0:T(8,128)(2,1)}), bf16[8,64,1,128]{3,1,2,0:T(8,128)(2,1)S(1)}, u32[]{:S(2)}, u32[]{:S(2)}) %all-to-all-start) | async-done | bytes 131104 | tf_op jit(solution)/shard_map/all_to_all | solution.py:32
  36.8 10.6 %all_to_all.20 = bf16[64,8,128]{2,0,1:T(8,128)(2,1)S(1)} all-to-all(bf16[64,8,128]{2,0,1:T(8,128)(2,1)S(1)} %select_bitcast_fusion), channel_id=1, replica_groups=mesh['dp'=8,'mp'=4] {'mp'}, dimensions={1} | all-to-all | bytes 262144 | tf_op jit(solution)/shard_map/all_to_all | solution.py:35
  47.6 0.9 convolution_convert_fusion.1
  49.2 32.3 %all-reduce.3.cloned.1.call-done = bf16[256,512]{1,0:T(8,128)(2,1)} async-done(((bf16[256,512]{1,0:T(8,128)(2,1)}), bf16[256,512]{1,0:T(8,128)(2,1)}) %all-reduce.3.cloned.1.call-update) | async-done | bytes 262160 | tf_op jit(solution)/shard_map/psum | solution.py:45
  81.5 1.2 fusion.6
  82.8 0.9 convolution_convert_fusion
  84.3 35.0 %all-reduce.5.cloned.1.call-done = bf16[256,512]{1,0:T(8,128)(2,1)} async-done(((bf16[256,512]{1,0:T(8,128)(2,1)}), bf16[256,512]{1,0:T(8,128)(2,1)}) %all-reduce.5.cloned.1.call-update) | async-done | bytes 262160 | tf_op jit(solution)/shard_map/psum | solution.py:45
  119.3 1.2 fusion.7
  120.6 16.0 %all_gather.6 = bf16[256,1024]{1,0:T(8,128)(2,1)S(1)} all-gather(bf16[256,256]{1,0:T(8,128)(2,1)S(1)} %fusion.7), channel_id=1, replica_groups=mesh['dp'=8,'mp'=4] {'mp'}, dimensions={1}, use_global_device_ids=true | all-gather | bytes 655360 | tf_op jit(solution)/shard_map/all_gather | solution.py:55
  136.5 2.4 %fusion.1 = bf16[256,512]{1,0:T(8,128)(2,1)} fusion(bf16[256,1024]{1,0:T(8,128)(2,1)S(1)} %all_gather.6, bf16[1024,512]{1,0:T(8,128)(2,1)} %all-gather.2.cloned.1.call-done, f32[512]{0:T(512)S(1)} %copy-done.4), kind=kOutput, calls=%fused_computation.11 | convolution fusion | flops 268828672 | bytes 1837056 | tf_op jit(solution)/shard_map/dot_general | solution.py:56
  (50 shorter events, 5.4 us)
Async XLA Ops:
  7.4 1.4 copy-start
  25.3 5.4 %copy-start.5 = (s32[8]{0:T(128)S(1)}, s32[8]{0:T(128)}, u32[]{:S(2)}) copy-start(s32[8]{0:T(128)} %param.12) | copy-start | bytes 100
  25.3 10.8 %all-to-all-start = ((bf16[8,64,1,128]{3,1,2,0:T(8,128)(2,1)}), bf16[8,64,1,128]{3,1,2,0:T(8,128)(2,1)S(1)}, u32[]{:S(2)}, u32[]{:S(2)}) async-start(bf16[8,64,1,128]{3,1,2,0:T(8,128)(2,1)} %fusion.18), calls=%async_computation | async-start | bytes 262144 | tf_op jit(solution)/shard_map/all_to_all | solution.py:32
  30.6 50.9 %all-reduce.3.cloned.1.call-start = ((), (), s32[]{:S(2)}) async-start(), calls=%async_computation.2 | async-start | bytes 524288 | tf_op jit(solution)/shard_map/psum | solution.py:45
  36.1 11.5 %copy-start.1 = (bf16[2,256,512]{2,1,0:T(8,128)(2,1)S(1)}, bf16[2,256,512]{2,1,0:T(8,128)(2,1)}, u32[]{:S(2)}) copy-start(bf16[2,256,512]{2,1,0:T(8,128)(2,1)} %param.13) | copy-start | bytes 1572868
  47.5 34.0 %copy-start.3 = (bf16[2,256,512]{2,1,0:T(8,128)(2,1)S(1)}, bf16[2,256,512]{2,1,0:T(8,128)(2,1)}, u32[]{:S(2)}) copy-start(bf16[2,256,512]{2,1,0:T(8,128)(2,1)} %param.14) | copy-start | bytes 1572868
  48.5 0.7 copy-start.2
  48.5 70.8 %all-reduce.5.cloned.1.call-start = ((), (), s32[]{:S(2)}) async-start(), calls=%async_computation.3 | async-start | bytes 524288 | tf_op jit(solution)/shard_map/psum | solution.py:45
  83.7 52.8 %all-gather.2.cloned.1.call-start = ((), (), s32[]{:S(2)}) async-start(), calls=%async_computation.4 | async-start | bytes 1179648 | tf_op jit(solution)/shard_map/all_gather | solution.py:58
  120.6 16.0 %copy-start.4 = (f32[512]{0:T(512)S(1)}, f32[512]{0:T(512)}, u32[]{:S(2)}) copy-start(f32[512]{0:T(512)} %param.17) | copy-start | bytes 6148
Sparse Core Ops, SparseCore 0:
  48.7 32.8 all-reduce.2
  83.9 35.4 all-reduce.4
Sparse Core Ops, SparseCore 1:
  86.1 23.1 all-gather.1
